TPU v7x, 32 devices: a whole 2x2x4 slice. The times are simulated.
32 devices in a mesh: groups: 2 (over y), seq: 4 (over z), batch: 4 (over x, core).
Axes of the slice: x: 2, y: 2, z: 4, core: 2. Of those that a mesh axis runs over, the one named last changes fastest.
Arguments:
- queries: bfloat16 [8, 512, 2048], P(('groups', 'batch'), 'seq'), parts along dimension 0, may hold values from -80 to 80, as said below
- keys: bfloat16 [8, 512, 512], P(('groups', 'batch'), 'seq'), parts along dimension 0, may hold values from -4.5 to 4.5
- values: bfloat16 [8, 512, 512], P(('groups', 'batch'), 'seq'), parts along dimension 0, may hold values from -6 to 6
Outputs:
- attended: bfloat16 [8, 512, 2048], P(('groups', 'batch'), 'seq'), parts along dimension 0
There are 2 independent parts, one for each index of `groups`. A program takes and returns all parts, laid end to end along the dimension named above; each array names one. Nothing has to cross between parts.
Inputs may be any that keep to these rules, and one draw needn't show every extreme that they name: `queries`: query vectors of order a few units; a few positions may hold much larger entries.
All inputs are finite; a program needn't handle non-finite values.
Results may differ from a plain program's by a relative error of at most 0.009.
Values may be sent and summed in bfloat16 or wider, within the bound.
A program may use at most 64 MiB of HBM per device.

v0:
```python
import math

import jax
import jax.numpy as jnp
from jax import lax
from jax.sharding import PartitionSpec as P

QUERY_HEADS = 16
KEY_VALUE_HEADS = 4
HEAD_SIZE = 128


def fresh_state(rows_per_half):
    query_heads_per_group = QUERY_HEADS // KEY_VALUE_HEADS
    current_maximum = jnp.full(
        (rows_per_half, KEY_VALUE_HEADS, query_heads_per_group), -1e30, jnp.float32
    )
    current_sum = jnp.zeros((rows_per_half, KEY_VALUE_HEADS, query_heads_per_group), jnp.float32)
    weighted_values = jnp.zeros(
        (rows_per_half, KEY_VALUE_HEADS, query_heads_per_group, HEAD_SIZE), jnp.float32
    )
    return (current_maximum, current_sum, weighted_values)


def update_state(state, query_half, positions, key_portion, value_portion, start):
    current_maximum, current_sum, weighted_values = state
    portion_rows = key_portion.shape[0]
    heads_of_keys = key_portion.reshape(portion_rows, KEY_VALUE_HEADS, HEAD_SIZE)
    heads_of_values = value_portion.reshape(portion_rows, KEY_VALUE_HEADS, HEAD_SIZE)
    scores = jnp.einsum(
        "qkgd,pkd->qkgp", query_half, heads_of_keys, preferred_element_type=jnp.float32
    )
    scores = scores * (1.0 / math.sqrt(HEAD_SIZE))
    key_pos = start + jnp.arange(portion_rows, dtype=jnp.int32)
    visible = (key_pos[None, :] <= positions[:, None])[:, None, None, :]
    new_max = jnp.maximum(current_maximum, jnp.max(jnp.where(visible, scores, -1e30), axis=-1))
    exp_scores = jnp.where(visible, jnp.exp(scores - new_max[..., None]), 0.0)
    rescale = jnp.exp(current_maximum - new_max)
    current_sum = current_sum * rescale + jnp.sum(exp_scores, axis=-1)
    weighted_values = weighted_values * rescale[..., None] + jnp.einsum(
        "qkgp,pkd->qkgd",
        exp_scores.astype(jnp.bfloat16),
        heads_of_values,
        preferred_element_type=jnp.float32,
    )
    return (new_max, current_sum, weighted_values)


def sweep_piece(state, query_half, positions, key_portion, value_portion, start):
    portion_rows = key_portion.shape[0]
    if portion_rows > 512 and portion_rows % 512 == 0:
        count = portion_rows // 512
        key_blocks = key_portion.reshape(count, 512, key_portion.shape[1])
        value_blocks = value_portion.reshape(count, 512, value_portion.shape[1])
        block_starts = start + 512 * jnp.arange(count, dtype=jnp.int32)

        def one_block(inner, block_args):
            return (
                update_state(
                    inner, query_half, positions, block_args[0], block_args[1], block_args[2]
                ),
                None,
            )

        state, _ = lax.scan(one_block, state, (key_blocks, value_blocks, block_starts))
        return state
    return update_state(state, query_half, positions, key_portion, value_portion, start)


def absorb_piece(states, halves, key_portion, value_portion, start):
    updated = []
    for state, (query_half, positions) in zip(states, halves):
        needed = jnp.logical_and(True, start <= positions[-1])
        updated.append(
            lax.cond(
                needed,
                lambda inner: sweep_piece(
                    inner, query_half, positions, key_portion, value_portion, start
                ),
                lambda inner: inner,
                state,
            )
        )
    return tuple(updated)


def finish_state(state, rows_per_half):
    current_maximum, current_sum, weighted_values = state
    return (
        (weighted_values / current_sum[..., None])
        .reshape(rows_per_half, QUERY_HEADS * HEAD_SIZE)
        .astype(jnp.bfloat16)
    )


def on_device(queries, keys, values):
    my_index = lax.axis_index("seq")
    token_rows = queries.shape[1]
    rows_per_half = token_rows // 2
    query_heads_per_group = QUERY_HEADS // KEY_VALUE_HEADS
    local_queries = queries[0].reshape(
        token_rows, KEY_VALUE_HEADS, query_heads_per_group, HEAD_SIZE
    )
    first_pos = my_index * token_rows + jnp.arange(rows_per_half, dtype=jnp.int32)
    second_pos = first_pos + rows_per_half
    first_half = local_queries[:rows_per_half]
    second_half = local_queries[rows_per_half:]
    halves = ((first_half, first_pos), (second_half, second_pos))
    states = (fresh_state(rows_per_half), fresh_state(rows_per_half))
    local_keys = keys[0]
    own_values = values[0]
    states = absorb_piece(
        states,
        halves,
        lax.all_gather(local_keys, "seq", axis=0, tiled=True),
        lax.all_gather(own_values, "seq", axis=0, tiled=True),
        jnp.int32(0),
    )
    first_out = finish_state(states[0], rows_per_half)
    second_out = finish_state(states[1], rows_per_half)
    return jnp.concatenate([first_out, second_out], axis=0)[None]


def solution(mesh):
    in_specs = (
        P(("groups", "batch"), "seq", None),
        P(("groups", "batch"), "seq", None),
        P(("groups", "batch"), "seq", None),
    )
    out_specs = P(("groups", "batch"), "seq", None)
    return jax.shard_map(
        on_device, mesh=mesh, in_specs=in_specs, out_specs=out_specs, check_vma=False
    )
```

profile of v0, /device:TPU:0, one launch (start us, length us, event | category | flops | bytes accessed | tf_op | source)
XLA Modules:
  0.0 51.1 jit_solution(15241243915679586384)
XLA Ops:
  0.0 0.6 %slice.21 = s32[1]{0:T(128)} slice(s32[64]{0:T(128)S(1)} %get-tuple-element.50), slice={[63:64]} | slice | bytes 8 | tf_op jit(solution)/shard_map/slice | solution.py:73
  1.2 17.6 %all-gather = bf16[1,512,512]{2,1,0:T(8,128)(2,1)S(1)} all-gather(bf16[1,128,512]{2,1,0:T(8,128)(2,1)} %param.8), channel_id=2, replica_groups=mesh['groups'=2,'seq'=4,'batch'=4] {'seq'}, dimensions={1}, use_global_device_ids=true | all-gather | bytes 655360 | tf_op jit(solution)/shard_map/all_gather | solution.py:115
  18.8 16.6 %all-gather.1 = bf16[1,512,512]{2,1,0:T(8,128)(2,1)S(1)} all-gather(bf16[1,128,512]{2,1,0:T(8,128)(2,1)} %param.9), channel_id=3, replica_groups=mesh['groups'=2,'seq'=4,'batch'=4] {'seq'}, dimensions={1}, use_global_device_ids=true | all-gather | bytes 655360 | tf_op jit(solution)/shard_map/all_gather | solution.py:116
  35.4 6.4 %conditional.3 = (f32[64,4,4]{0,2,1:T(4,128)S(1)}, f32[64,4,4,128]{3,0,2,1:T(8,128)S(1)}) conditional(s32[]{:T(128)} %bitcast.11, () %tuple.23, (s32[64]{0:T(128)S(1)}, bf16[512,512]{1,0:T(8,128)(2,1)S(1)}, bf16[1,128,2048]{2,1,0:T(8,128)(2,1)}, bf16[512,512]{1,0:T(8,128)(2,1)S(1)}) %tuple.36), branch_computations={%region_4.5_spmd, %region_5.8_spmd} | conditional | flops 274369536 | bytes 19837228 | solution.py:75
  35.4 0.1 iota_compare_fusion.1
  35.5 1.0 %slice.16 = bf16[1,64,2048]{2,1,0:T(8,128)(2,1)S(1)} slice(bf16[1,128,2048]{2,1,0:T(8,128)(2,1)} %get-tuple-element.31), slice={[0:1], [64:128], [0:2048]} | slice | bytes 524288 | tf_op jit(solution)/shard_map/slice | solution.py:107
  36.5 0.2 slice.17
  36.6 0.1 reshape.76
  36.8 0.6 %fusion.18 = (f32[64,4,4]{0,2,1:T(4,128)S(1)}, f32[4,512,64,4]{1,2,3,0:T(8,128)S(1)}) fusion(pred[64,512]{1,0:T(8,128)(4,1)S(1)} %iota_compare_fusion.1, bf16[64,4,4,128]{3,2,1,0:T(4,128)(2,1)S(1)} %slice.17, bf16[512,4,128,1]{2,1,0,3:T(4,128)(2,1)S(1)} %bitcast.52), kind=kOutput, calls=%fused_computation.25 | convolution fusion | flops 135789568 | bytes 2920448 | tf_op jit(solution)/shard_map/cond/branch_1_fun/qkgd,pkd->qkgp/dot_general | solution.py:30
  37.3 0.0 copy-start
  37.4 1.3 %copy-done = f32[4,512,64,4]{1,2,3,0:T(8,128)} copy-done((f32[4,512,64,4]{1,2,3,0:T(8,128)}, f32[4,512,64,4]{1,2,3,0:T(8,128)S(1)}, u32[]{:S(2)}) %copy-start) | copy-done | bytes 2097176 | tf_op jit(solution)/shard_map/cond
  38.7 0.7 %fusion.22 = f32[64,4,4]{0,2,1:T(4,128)S(1)} fusion(f32[4,512,64,4]{1,2,3,0:T(8,128)S(1)} %get-tuple-element.48, f32[64,4,4]{0,2,1:T(4,128)S(1)} %broadcast_maximum_fusion.1, pred[64,512]{1,0:T(8,128)(4,1)S(1)} %iota_compare_fusion.1), kind=kLoop, calls=%fused_computation.29 | loop fusion | flops 2096128 | bytes 2138112 | tf_op jit(solution)/shard_map/cond/branch_1_fun/reduce_sum | solution.py:39
  39.4 0.1 reshape.77
  39.5 2.3 %fusion.23 = f32[64,4,4,128]{3,0,2,1:T(8,128)S(1)} fusion(f32[4,512,64,4]{1,2,3,0:T(8,128)} %copy-done, f32[64,4,4]{0,2,1:T(4,128)S(1)} %broadcast_maximum_fusion.1, pred[64,512]{1,0:T(8,128)(4,1)S(1)} %iota_compare_fusion.1, bf16[512,4,128,1]{2,1,0,3:T(4,128)(2,1)S(1)} %bitcast.50, f32[64,4,4]{0,2,1:T(4,128)S(1)} %get-tuple-element.45), kind=kOutput, calls=%fused_computation.31 | convolution fusion | flops 136445952 | bytes 3186688 | tf_op jit(solution)/shard_map/cond/branch_1_fun/qkgp,pkd->qkgd/dot_general | solution.py:40
  41.8 0.2 divide_convert_fusion
  42.0 0.2 copy.17
  42.2 0.2 convert_element_type.37
  42.4 0.6 %slice.20 = s32[1]{0:T(128)} slice(s32[64]{0:T(128)S(1)} %get-tuple-element.49), slice={[63:64]} | slice | bytes 8 | tf_op jit(solution)/shard_map/slice | solution.py:73
  43.6 6.0 %conditional.2 = (f32[64,4,4]{0,2,1:T(4,128)S(1)}, f32[64,4,4,128]{3,0,2,1:T(8,128)S(1)}) conditional(s32[]{:T(128)} %bitcast.8, () %tuple.21, (s32[64]{0:T(128)S(1)}, bf16[512,512]{1,0:T(8,128)(2,1)S(1)}, bf16[1,128,2048]{2,1,0:T(8,128)(2,1)}, bf16[512,512]{1,0:T(8,128)(2,1)S(1)}) %tuple.37), branch_computations={%region_0.0_spmd, %region_1.4_spmd} | conditional | flops 274369536 | bytes 11448592 | solution.py:75
  43.6 0.1 iota_compare_fusion
  43.7 1.0 %slice.14 = bf16[1,64,2048]{2,1,0:T(8,128)(2,1)S(1)} slice(bf16[1,128,2048]{2,1,0:T(8,128)(2,1)} %get-tuple-element.27), slice={[0:1], [0:64], [0:2048]} | slice | bytes 524288 | tf_op jit(solution)/shard_map/slice | solution.py:106
  44.7 0.9 %slice.15 = bf16[64,4,4,128]{3,2,1,0:T(4,128)(2,1)} reshape(bf16[1,64,2048]{2,1,0:T(8,128)(2,1)S(1)} %slice.14) | data formatting | bytes 524288 | tf_op jit(solution)/shard_map/slice | solution.py:106
  45.6 0.9 %reshape.74 = bf16[512,4,128]{2,1,0:T(4,128)(2,1)} reshape(bf16[512,512]{1,0:T(8,128)(2,1)S(1)} %get-tuple-element.26) | data formatting | bytes 1048576 | tf_op jit(solution)/shard_map/cond/branch_1_fun/reshape | solution.py:28
  46.5 1.7 %fusion = (f32[64,4,4]{0,2,1:T(4,128)S(1)}, f32[4,512,64,4]{1,2,3,0:T(8,128)S(1)}) fusion(pred[64,512]{1,0:T(8,128)(4,1)S(1)} %iota_compare_fusion, bf16[64,4,4,128]{3,2,1,0:T(4,128)(2,1)} %slice.15, bf16[512,4,128,1]{2,1,0,3:T(4,128)(2,1)} %bitcast.53), kind=kOutput, calls=%fused_computation.2 | convolution fusion | flops 135789568 | bytes 2920448 | tf_op jit(solution)/shard_map/cond/branch_1_fun/qkgd,pkd->qkgp/dot_general | solution.py:30
  48.2 0.7 %fusion.4 = f32[64,4,4]{0,2,1:T(4,128)S(1)} fusion(f32[4,512,64,4]{1,2,3,0:T(8,128)S(1)} %get-tuple-element.44, f32[64,4,4]{0,2,1:T(4,128)S(1)} %broadcast_maximum_fusion, pred[64,512]{1,0:T(8,128)(4,1)S(1)} %iota_compare_fusion), kind=kLoop, calls=%fused_computation.6 | loop fusion | flops 2096128 | bytes 2138112 | tf_op jit(solution)/shard_map/cond/branch_1_fun/reduce_sum | solution.py:39
  48.9 0.1 reshape.75
  49.0 0.7 %fusion.5 = f32[64,4,4,128]{3,0,2,1:T(8,128)S(1)} fusion(f32[4,512,64,4]{1,2,3,0:T(8,128)S(1)} %get-tuple-element.44, f32[64,4,4]{0,2,1:T(4,128)S(1)} %broadcast_maximum_fusion, pred[64,512]{1,0:T(8,128)(4,1)S(1)} %iota_compare_fusion, bf16[512,4,128,1]{2,1,0,3:T(4,128)(2,1)S(1)} %bitcast.51, f32[64,4,4]{0,2,1:T(4,128)S(1)} %get-tuple-element.41), kind=kOutput, calls=%fused_computation.8 | convolution fusion | flops 136445952 | bytes 3186688 | tf_op jit(solution)/shard_map/cond/branch_1_fun/qkgp,pkd->qkgd/dot_general | solution.py:40
  49.7 0.2 divide_convert_fusion.1
  49.9 0.2 copy.16
  50.1 0.2 convert_element_type.33
  50.3 0.8 %maximum_bitcast_fusion = bf16[1,128,2048]{2,1,0:T(8,128)(2,1)} fusion(bf16[64,2048]{1,0:T(8,128)(2,1)S(1)} %convert_element_type.37, bf16[64,2048]{1,0:T(8,128)(2,1)S(1)} %convert_element_type.33), kind=kLoop, calls=%fused_computation.46 | loop fusion | flops 1048576 | bytes 1048576 | tf_op jit(solution)/shard_map/broadcast_in_dim | solution.py:121
  (5 shorter events, 0.0 us)
Async XLA Ops:
  37.3 1.4 %copy-start = (f32[4,512,64,4]{1,2,3,0:T(8,128)}, f32[4,512,64,4]{1,2,3,0:T(8,128)S(1)}, u32[]{:S(2)}) copy-start(f32[4,512,64,4]{1,2,3,0:T(8,128)S(1)} %get-tuple-element.48) | copy-start | bytes 6291460 | tf_op jit(solution)/shard_map/cond
where the time goes:
time: 51.4 us; the launch traced here: 51.1 us
  blocking collectives  34.1 us (66%)
  local copies, waits for them, and re-layouts  7.54 us (15%)
  matrix products  5.2 us (10%)
  other arithmetic  2.77 us (5%)
  between operations  1.36 us (3%)
    all_gather x1, blocking collectives, on_device(): lax.all_gather(local_keys, 'seq', axis=0, tiled=True)  17.6 us
    all_gather x1, blocking collectives, on_device(): lax.all_gather(own_values, 'seq', axis=0, tiled=True)  16.6 us
    dot_general x2, matrix products, update_state(): jnp.einsum('qkgp,pkd->qkgd', exp_scores.astype(jnp.bfloat16), heads_of_va...  2.95 us
    dot_general x2, matrix products, update_state(): jnp.einsum('qkgd,pkd->qkgp', query_half, heads_of_keys, preferred_element...  2.25 us
    slice x2, local copies, waits for them, and re-layouts, on_device(): first_half = local_queries[:rows_per_half]  1.83 us
    cond x2, local copies, waits for them, and re-layouts  1.34 us
    reduce_sum x2, other arithmetic, update_state(): current_sum = current_sum * rescale + jnp.sum(exp_scores, axis=-1)  1.31 us
    slice x2, local copies, waits for them, and re-layouts, absorb_piece(): needed = jnp.logical_and(True, start <= positions[-1])  1.17 us

commit v1 on v0

v1 whole, which is shorter than its diff:
```python
import functools
import math

import jax
import jax.numpy as jnp
from jax import lax
from jax.experimental import pallas as pl
from jax.experimental.pallas import tpu as pltpu
from jax.sharding import PartitionSpec as P

HEAD_SIZE = 128
SCALE = math.log2(math.e) / math.sqrt(HEAD_SIZE)
MESH = pl.DeviceIdType.MESH


def kernel(
    n, groups, per_group,
    q_hbm, k_hbm, v_hbm, o_hbm,
    q, kv, m, acc, o,
    load_sem, q_sem, o_sem, send_sem, recv_sem,
):
    rows = q.shape[0]
    me = lax.axis_index("seq")
    right, left = lax.rem(me + 1, n), lax.rem(me + n - 1, n)
    wide = per_group * HEAD_SIZE

    def loads(g):
        cols = pl.ds(g * HEAD_SIZE, HEAD_SIZE)
        return (
            pltpu.make_async_copy(
                k_hbm.at[0, :, cols], kv.at[0, g, pl.ds(0, rows)], load_sem.at[0, g]
            ),
            pltpu.make_async_copy(
                v_hbm.at[0, :, cols], kv.at[0, g, pl.ds(rows, rows)], load_sem.at[1, g]
            ),
        )

    def send(slot, g):
        return pltpu.make_async_remote_copy(
            src_ref=kv.at[slot, g],
            dst_ref=kv.at[slot + 1, g],
            send_sem=send_sem.at[slot, g],
            recv_sem=recv_sem.at[slot + 1, g],
            device_id={"seq": right},
            device_id_type=MESH,
        )

    def receive(slot, g):
        return pltpu.make_async_remote_copy(
            src_ref=kv.at[slot, g],
            dst_ref=kv.at[slot, g],
            send_sem=send_sem.at[slot, g],
            recv_sem=recv_sem.at[slot, g],
            device_id={"seq": right},
            device_id_type=MESH,
        )

    def out_copy(g):
        cols = pl.ds(g * wide, wide)
        return pltpu.make_async_copy(o.at[:, cols], o_hbm.at[0, :, cols], o_sem.at[g])

    q_copy = pltpu.make_async_copy(q_hbm.at[0], q, q_sem)

    barrier = pltpu.get_barrier_semaphore()

    @pl.when(me > 0)
    def _():
        pl.semaphore_signal(barrier, inc=1, device_id={"seq": left}, device_id_type=MESH)

    for g in range(groups):
        for copy in loads(g):
            copy.start()
    q_copy.start()

    @pl.when(me < n - 1)
    def _():
        pl.semaphore_wait(barrier, 1)

    for g in range(groups):
        for copy in loads(g):
            copy.wait()

        @pl.when(me < n - 1)
        def _():
            send(0, g).start()

    q_copy.wait()

    def scores_of(slot, g):
        stacked = jnp.concatenate(
            [
                q[:, (g * per_group + h) * HEAD_SIZE : (g * per_group + h + 1) * HEAD_SIZE]
                for h in range(per_group)
            ],
            axis=0,
        )
        return lax.dot_general(
            stacked,
            kv[slot, g, :rows, :],
            (((1,), (1,)), ((), ())),
            preferred_element_type=jnp.float32,
        )

    def weighted(p, slot, g):
        block = jnp.concatenate(
            [kv[slot, g, rows:, :], jnp.ones((rows, HEAD_SIZE), jnp.bfloat16)], axis=1
        )
        return jnp.dot(p.astype(jnp.bfloat16), block, preferred_element_type=jnp.float32)

    def finish(total, g):
        done = (total[:, :HEAD_SIZE] / total[:, HEAD_SIZE:]).astype(jnp.bfloat16)
        for h in range(per_group):
            at = (g * per_group + h) * HEAD_SIZE
            o[:, at : at + HEAD_SIZE] = done[h * rows : (h + 1) * rows]
        out_copy(g).start()

    row = lax.rem(lax.broadcasted_iota(jnp.int32, (per_group * rows, rows), 0), rows)
    visible = lax.broadcasted_iota(jnp.int32, (per_group * rows, rows), 1) <= row

    for g in range(groups):
        s = jnp.where(visible, scores_of(0, g), -1e30)
        new_m = jnp.max(s, axis=1, keepdims=True)
        total = weighted(jnp.exp2((s - new_m) * SCALE), 0, g)
        acc[g] = total
        m[g] = jnp.broadcast_to(new_m, m.shape[1:])

        @pl.when(me == 0)
        def _():
            finish(acc[g], g)

    @pl.loop(1, me + 1)
    def _(slot):
        for g in range(groups):
            receive(slot, g).wait_recv()

            @pl.when(me < n - 1)
            def _():
                send(slot, g).start()

            s = scores_of(slot, g)
            old_m = m[g]
            new_m = jnp.maximum(old_m, jnp.max(s, axis=1, keepdims=True))
            fade = jnp.exp2((old_m - new_m) * SCALE)
            p = jnp.exp2((s - new_m[:, :1]) * SCALE)
            total = acc[g] * jnp.concatenate([fade, fade], axis=1) + weighted(p, slot, g)

            @pl.when(slot < me)
            def _():
                acc[g] = total
                m[g] = new_m

            @pl.when(slot == me)
            def _():
                finish(total, g)

    @pl.when(me < n - 1)
    def _():
        @pl.loop(0, me + 1)
        def _(slot):
            for g in range(groups):
                send(slot, g).wait_send()

    for g in range(groups):
        out_copy(g).wait()


def on_device(n, queries, keys, values):
    rows, query_width = queries.shape[1:]
    groups = keys.shape[2] // HEAD_SIZE
    per_group = query_width // HEAD_SIZE // groups
    hbm = pl.BlockSpec(memory_space=pl.ANY)
    return pl.pallas_call(
        functools.partial(kernel, n, groups, per_group),
        out_shape=jax.ShapeDtypeStruct(queries.shape, queries.dtype),
        in_specs=[hbm, hbm, hbm],
        out_specs=hbm,
        scratch_shapes=[
            pltpu.VMEM((rows, query_width), jnp.bfloat16),
            pltpu.VMEM((n, groups, 2 * rows, HEAD_SIZE), jnp.bfloat16),
            pltpu.VMEM((groups, per_group * rows, HEAD_SIZE), jnp.float32),
            pltpu.VMEM((groups, per_group * rows, 2 * HEAD_SIZE), jnp.float32),
            pltpu.VMEM((rows, query_width), jnp.bfloat16),
            pltpu.SemaphoreType.DMA((2, groups)),
            pltpu.SemaphoreType.DMA,
            pltpu.SemaphoreType.DMA((groups,)),
            pltpu.SemaphoreType.DMA((n, groups)),
            pltpu.SemaphoreType.DMA((n, groups)),
        ],
        compiler_params=pltpu.CompilerParams(collective_id=0, has_side_effects=True),
    )(queries, keys, values)


def solution(mesh):
    spec = P(("groups", "batch"), "seq", None)
    return jax.shard_map(
        functools.partial(on_device, mesh.shape["seq"]),
        mesh=mesh,
        in_specs=(spec, spec, spec),
        out_specs=spec,
        check_vma=False,
    )
```

time: 51.4 us -> 23 us (0.45)
  the two profiles are of different devices: /device:TPU:0 before, /device:TPU:24 now
where the time goes in v1:
time: 23 us; the launch traced here: 22.9 us
  Pallas kernels  21 us (91%)
  local copies, waits for them, and re-layouts  1.88 us (8%)
    pallas_call x1, Pallas kernels, on_device(): pl.pallas_call(functools.partial(kernel, n, groups, per_group), out_shape...  21 us
    unnamed x1, local copies, waits for them, and re-layouts  1.88 us

profile of v1, /device:TPU:24, one launch (start us, length us, event | category | flops | bytes accessed | tf_op | source)
XLA Modules:
  0.0 22.9 jit_solution(10825314741043252337)
XLA Ops:
  0.0 21.0 %shard_map.37 = bf16[1,128,2048]{2,1,0:T(8,128)(2,1)} custom-call(bf16[1,128,2048]{2,1,0:T(8,128)(2,1)} %q_hbm.1, bf16[1,128,512]{2,1,0:T(8,128)(2,1)} %k_hbm.1, bf16[1,128,512]{2,1,0:T(8,128)(2,1)} %v_hbm.1), custom_call_target="tpu_custom_call" | custom-call | tf_op jit(solution)/shard_map/pallas_call | solution.py:172
  21.0 1.9 %copy.5 = bf16[1,128,2048]{2,1,0:T(8,128)(2,1)} copy(bf16[1,128,2048]{2,1,0:T(8,128)(2,1)} %shard_map.37) | data formatting | bytes 1048576

commit v2 on v1

--- a/solution.py
+++ b/solution.py
@@ -15,14 +15,13 @@
 
 def kernel(
     n, groups, per_group,
-    q_hbm, k_hbm, v_hbm, o_hbm,
-    q, kv, m, acc, o,
-    load_sem, q_sem, o_sem, send_sem, recv_sem,
+    q_hbm, k_hbm, v_hbm, o,
+    q, kv, m, acc,
+    load_sem, q_sem, send_sem, recv_sem,
 ):
     rows = q.shape[0]
     me = lax.axis_index("seq")
     right, left = lax.rem(me + 1, n), lax.rem(me + n - 1, n)
-    wide = per_group * HEAD_SIZE
 
     def loads(g):
         cols = pl.ds(g * HEAD_SIZE, HEAD_SIZE)
@@ -54,10 +53,6 @@
             device_id={"seq": right},
             device_id_type=MESH,
         )
-
-    def out_copy(g):
-        cols = pl.ds(g * wide, wide)
-        return pltpu.make_async_copy(o.at[:, cols], o_hbm.at[0, :, cols], o_sem.at[g])
 
     q_copy = pltpu.make_async_copy(q_hbm.at[0], q, q_sem)
 
@@ -111,8 +106,7 @@
         done = (total[:, :HEAD_SIZE] / total[:, HEAD_SIZE:]).astype(jnp.bfloat16)
         for h in range(per_group):
             at = (g * per_group + h) * HEAD_SIZE
-            o[:, at : at + HEAD_SIZE] = done[h * rows : (h + 1) * rows]
-        out_copy(g).start()
+            o[0, :, at : at + HEAD_SIZE] = done[h * rows : (h + 1) * rows]
 
     row = lax.rem(lax.broadcasted_iota(jnp.int32, (per_group * rows, rows), 0), rows)
     visible = lax.broadcasted_iota(jnp.int32, (per_group * rows, rows), 1) <= row
@@ -160,34 +154,30 @@
             for g in range(groups):
                 send(slot, g).wait_send()
 
-    for g in range(groups):
-        out_copy(g).wait()
-
 
 def on_device(n, queries, keys, values):
     rows, query_width = queries.shape[1:]
     groups = keys.shape[2] // HEAD_SIZE
     per_group = query_width // HEAD_SIZE // groups
-    hbm = pl.BlockSpec(memory_space=pl.ANY)
+    hbm = pl.BlockSpec(memory_space=pltpu.HBM)
+    held = (2 * rows * query_width + 2 * n * rows * keys.shape[2]) * 2 + 3 * rows * query_width * 4
     return pl.pallas_call(
         functools.partial(kernel, n, groups, per_group),
         out_shape=jax.ShapeDtypeStruct(queries.shape, queries.dtype),
         in_specs=[hbm, hbm, hbm],
-        out_specs=hbm,
+        out_specs=pl.BlockSpec(memory_space=pltpu.VMEM),
         scratch_shapes=[
             pltpu.VMEM((rows, query_width), jnp.bfloat16),
             pltpu.VMEM((n, groups, 2 * rows, HEAD_SIZE), jnp.bfloat16),
             pltpu.VMEM((groups, per_group * rows, HEAD_SIZE), jnp.float32),
             pltpu.VMEM((groups, per_group * rows, 2 * HEAD_SIZE), jnp.float32),
-            pltpu.VMEM((rows, query_width), jnp.bfloat16),
             pltpu.SemaphoreType.DMA((2, groups)),
             pltpu.SemaphoreType.DMA,
-            pltpu.SemaphoreType.DMA((groups,)),
             pltpu.SemaphoreType.DMA((n, groups)),
             pltpu.SemaphoreType.DMA((n, groups)),
         ],
-        compiler_params=pltpu.CompilerParams(collective_id=0, has_side_effects=True),
-    )(queries, keys, values)
+        compiler_params=pltpu.CompilerParams(collective_id=0, has_side_effects=True, vmem_limit_bytes=held + 4 * 2**20),
+    )(*(pltpu.with_memory_space_constraint(x, pltpu.HBM) for x in (queries, keys, values)))
 
 
 def solution(mesh):

time: 23 us -> 21.2 us (0.922)
  local copies, waits for them, and re-layouts: 1.88 us -> 0.8 us
  Pallas kernels: 21 us -> 20.3 us
    unnamed x1, local copies, waits for them, and re-layouts: 1.88 us -> 0.8 us
    pallas_call x1, Pallas kernels: 21 us -> 20.3 us  [on_device(): pl.pallas_call(functools.partial(kernel, n, groups, per_group), out_shape...]
where the time goes in v2:
time: 21.2 us; the launch traced here: 21.1 us
  Pallas kernels  20.3 us (96%)
  local copies, waits for them, and re-layouts  0.8 us (4%)
    pallas_call x1, Pallas kernels, on_device(): pl.pallas_call(functools.partial(kernel, n, groups, per_group), out_shape...  20.3 us
    unnamed x1, local copies, waits for them, and re-layouts  0.8 us

profile of v2, /device:TPU:24, one launch (start us, length us, event | category | flops | bytes accessed | tf_op | source)
XLA Modules:
  0.0 21.1 jit_solution(12497606741375655877)
XLA Ops:
  0.0 20.3 %shard_map.37 = bf16[1,128,2048]{2,1,0:T(8,128)(2,1)S(1)} custom-call(bf16[1,128,2048]{2,1,0:T(8,128)(2,1)} %q_hbm.1, bf16[1,128,512]{2,1,0:T(8,128)(2,1)} %k_hbm.1, bf16[1,128,512]{2,1,0:T(8,128)(2,1)} %v_hbm.1), custom_call_target="tpu_custom_call" | custom-call | tf_op jit(solution)/shard_map/pallas_call | solution.py:164
  20.3 0.8 %copy.5 = bf16[1,128,2048]{2,1,0:T(8,128)(2,1)} copy(bf16[1,128,2048]{2,1,0:T(8,128)(2,1)S(1)} %shard_map.37) | data formatting | bytes 1048576
